TPU v7x, 32 devices: a whole 2x2x4 slice. The times are simulated.
32 devices in a mesh: ctx: 8 (over y, x, core), fsdp: 4 (over z).
Axes of the slice: x: 2, y: 2, z: 4, core: 2. Of those that a mesh axis runs over, the one named last changes fastest.
Arguments:
- inputs: bfloat16 [4, 1024, 1536], P('fsdp', 'ctx')
- positions: int32 [4, 1024], P('fsdp', 'ctx'), may hold values from 0 to 1535, as said below
- block_order: int32 [16], replicated, may hold values from 0 to 15, as said below
- attention_gain: bfloat16 [1536], P('fsdp'), may hold values from 0.5 to 1.5
- projection: bfloat16 [1536, 2048], P('fsdp')
- projection_bias: bfloat16 [2048], P('fsdp'), may hold values from -4 to 4
- output_weight: bfloat16 [1536, 1536], P('fsdp'), may hold values from -1.5 to 1.5
- feedforward_gain: bfloat16 [1536], P('fsdp'), may hold values from 0.5 to 1.5
- gate_up: bfloat16 [1536, 17920], P('fsdp'), may hold values from -0.15625 to 0.15625
- down_weight: bfloat16 [8960, 1536], P('fsdp'), may hold values from -0.0625 to 0.0625
- cotangent: bfloat16 [4, 1024, 1536], P('fsdp', 'ctx'), may hold values from -6 to 6
Outputs:
- outputs: bfloat16 [4, 1024, 1536], P('fsdp', 'ctx')
- gradient: bfloat16 [4, 1024, 1536], P('fsdp', 'ctx')
- gradient_attention_gain: float32 [1536], P(('ctx', 'fsdp'))
- gradient_projection: float32 [1536, 2048], P('fsdp', 'ctx')
- gradient_projection_bias: float32 [2048], P(('ctx', 'fsdp'))
- gradient_output: float32 [1536, 1536], P('fsdp', 'ctx')
- gradient_feedforward_gain: float32 [1536], P(('ctx', 'fsdp'))
- gradient_gate_up: float32 [1536, 17920], P('fsdp', 'ctx')
- gradient_down: float32 [8960, 1536], P('fsdp', 'ctx')
Inputs may be any that keep to these rules, and one draw needn't show every extreme that they name: `block_order`: A permutation: each of 0 to 15 appears once. Within each sequence, positions grow strictly with order_index; the sequence's first token has position 0, and of the 1023 steps between tokens next to each other in the sequence exactly 512 are 2 and the others are 1, so the last token has position 1535.
All inputs are finite; a program needn't handle non-finite values.
Results may differ from a plain program's by a relative error of at most 0.02.
Values may be sent and summed in bfloat16 or wider, within the bound.
A program may use at most 320 MiB of HBM per device.

v0:
```python
import math

import jax
import jax.numpy as jnp
from jax import lax
from jax.sharding import PartitionSpec as P

HEADS = 12
KV_HEADS = 2
HEAD = 128
FF = 8960


EPS = 1e-06
THETA = 1000000.0
NEGATIVE = -1e30


def passed_along(block, axis, distance):
    devices = range(lax.axis_size(axis))
    route = [((i - distance) % len(devices), i) for i in devices]
    return lax.ppermute(block, axis, route)


def rope_tables(places):
    freq = THETA ** (-jnp.arange(0, HEAD, 2).astype(jnp.float32) / HEAD)
    angle = places.astype(jnp.float32)[:, None] * freq[None, :]
    angle = jnp.concatenate([angle, angle], axis=-1)
    return (jnp.cos(angle), jnp.sin(angle))


def rotate(values):
    middle = values.shape[-1] // 2
    return jnp.concatenate([-values[..., middle:], values[..., :middle]], axis=-1)


def apply_rope(values, cosine, sine):
    return values * cosine[:, None, :] + rotate(values) * sine[:, None, :]


def rope_back(grads, cosine, sine):
    return grads * cosine[:, None, :] - rotate(grads * sine[:, None, :])


def order_rows(block_order, start, count, half):
    offsets = start + jnp.arange(count, dtype=jnp.int32)
    slots = offsets // half
    table = jnp.arange(block_order.shape[0], dtype=jnp.int32)
    picked = jnp.sum(jnp.where(slots[:, None] == table[None, :], block_order[None, :], 0), axis=1)
    return picked * half + offsets % half


def rms_inverse(values):
    return lax.rsqrt(jnp.mean(values * values, axis=-1, keepdims=True) + EPS)


def norm_back(d_normed, values, inverse, gain):
    unit = values * inverse
    d_unit = d_normed * gain
    d_gain = jnp.sum(d_normed * unit, axis=0)
    d_values = inverse * (d_unit - unit * jnp.mean(d_unit * unit, axis=-1, keepdims=True))
    return (d_values, d_gain)


def contract_rows(left, right):
    return lax.dot_general(
        left, right, (((0,), (0,)), ((), ())), preferred_element_type=jnp.float32
    )


def contract_columns(left, right):
    return lax.dot_general(
        left, right, (((1,), (1,)), ((), ())), preferred_element_type=jnp.float32
    )


def score_block(queries, query_index, keys_values, key_index):
    split = keys_values.shape[1] // 2
    groups = queries.shape[0]
    size = queries.shape[2]
    keys = keys_values[:, :split].reshape(-1, groups, size)
    values = keys_values[:, split:].reshape(-1, groups, size)
    scores = jnp.einsum("grd,kgd->grk", queries, keys, preferred_element_type=jnp.float32) * (
        1.0 / math.sqrt(size)
    )
    mask = key_index[None, :] <= query_index[:, None]
    return (scores, mask[None, :, :], keys, values)


def forward_update(state, queries, query_index, keys_values, key_index):
    running_max, running_sum, accum = state
    scores, mask, keys, values = score_block(queries, query_index, keys_values, key_index)
    scores = jnp.where(mask, scores, NEGATIVE)
    new_max = jnp.maximum(running_max, jnp.max(scores, axis=-1))
    factor = jnp.exp(running_max - new_max)
    weights = jnp.where(mask, jnp.exp(scores - new_max[..., None]), 0.0)
    accum = accum * factor[..., None] + jnp.einsum(
        "grk,kgd->grd", weights.astype(jnp.bfloat16), values, preferred_element_type=jnp.float32
    )
    running_sum = running_sum * factor + jnp.sum(weights, axis=-1)
    return (new_max, running_sum, accum)


def backward_update(
    d_queries, d_pairs, queries, query_index, keys_values, key_index, d_attention, logsum, delta
):
    scores, mask, keys, values = score_block(queries, query_index, keys_values, key_index)
    scale = 1.0 / math.sqrt(queries.shape[2])
    probs = jnp.where(mask, jnp.exp(scores - logsum[..., None]), 0.0)
    d_values = jnp.einsum(
        "grk,grd->kgd", probs.astype(jnp.bfloat16), d_attention, preferred_element_type=jnp.float32
    )
    d_probs = jnp.einsum("grd,kgd->grk", d_attention, values, preferred_element_type=jnp.float32)
    d_scores = (probs * (d_probs - delta[..., None])).astype(jnp.bfloat16)
    d_queries = (
        d_queries
        + jnp.einsum("grk,kgd->grd", d_scores, keys, preferred_element_type=jnp.float32) * scale
    )
    d_keys = (
        jnp.einsum("grk,grd->kgd", d_scores, queries, preferred_element_type=jnp.float32) * scale
    )
    count = keys_values.shape[0]
    d_pairs = d_pairs + jnp.concatenate(
        [d_keys.reshape(count, -1), d_values.reshape(count, -1)], axis=1
    )
    return (d_queries, d_pairs)


def send_back(pairs):
    return passed_along(pairs.astype(jnp.bfloat16), "ctx", 1).astype(pairs.dtype)


def attention_params(attention_gain, projection, projection_bias, output_weight):
    return (
        lax.all_gather(attention_gain, "fsdp", axis=0, tiled=True),
        lax.all_gather(projection, "fsdp", axis=0, tiled=True),
        lax.all_gather(projection_bias, "fsdp", axis=0, tiled=True),
        lax.all_gather(output_weight, "fsdp", axis=0, tiled=True),
    )


def feedforward_params(feedforward_gain, gate_up, down_weight):
    return (
        lax.all_gather(feedforward_gain, "fsdp", axis=0, tiled=True),
        lax.all_gather(gate_up, "fsdp", axis=0, tiled=True),
        lax.all_gather(down_weight, "fsdp", axis=0, tiled=True),
    )


def owner_rows(left, right):
    slices = lax.all_to_all(left, "fsdp", split_axis=1, concat_axis=0, tiled=True)
    return contract_rows(slices, lax.all_gather(right, "fsdp", axis=0, tiled=True))


def body(
    inputs,
    positions,
    block_order,
    attention_gain,
    projection,
    projection_bias,
    output_weight,
    feedforward_gain,
    gate_up,
    down_weight,
    cotangent,
):
    rows = inputs.shape[1]
    half = rows // 2
    groups = KV_HEADS
    ratio = HEADS // KV_HEADS
    size = HEAD
    query_width = HEADS * HEAD
    key_width = KV_HEADS * HEAD
    cycle = lax.axis_size("ctx")
    place = lax.axis_index("ctx")
    whole_gain, whole_projection, whole_bias, whole_output = attention_params(
        attention_gain, projection, projection_bias, output_weight
    )
    features = inputs[0].astype(jnp.float32)
    inverse_one = rms_inverse(features)
    normed_one = (features * inverse_one * whole_gain.astype(jnp.float32)).astype(jnp.bfloat16)
    projected = jnp.dot(
        normed_one, whole_projection, preferred_element_type=jnp.float32
    ) + whole_bias.astype(jnp.float32)
    cosine, sine = rope_tables(positions[0])
    queries = apply_rope(
        projected[:, :query_width].reshape(rows, HEADS, size), cosine, sine
    ).astype(jnp.bfloat16)
    keys = apply_rope(
        projected[:, query_width : query_width + key_width].reshape(rows, groups, size),
        cosine,
        sine,
    ).astype(jnp.bfloat16)
    values = projected[:, query_width + key_width :].astype(jnp.bfloat16)
    keys_values = jnp.concatenate([keys.reshape(rows, key_width), values], axis=1)
    grouped = (
        queries.reshape(rows, groups, ratio, size)
        .transpose(1, 0, 2, 3)
        .reshape(groups, rows * ratio, size)
    )
    own_index = order_rows(block_order, place * rows, rows, half)
    query_index = jnp.repeat(own_index, ratio)
    start_state = (
        jnp.full((groups, rows * ratio), NEGATIVE, jnp.float32),
        jnp.zeros((groups, rows * ratio), jnp.float32),
        jnp.zeros((groups, rows * ratio, size), jnp.float32),
    )
    state = forward_update(start_state, grouped, query_index, keys_values, own_index)

    def forward_turn(turn, carry):
        state, held = carry
        held = passed_along(held, "ctx", 1)
        source = (place - turn) % cycle
        state = forward_update(
            state, grouped, query_index, held, order_rows(block_order, source * rows, rows, half)
        )
        return (state, held)

    state, held = lax.fori_loop(1, cycle, forward_turn, (state, keys_values))
    running_max, running_sum, accum = state
    attention = accum / running_sum[..., None]
    logsum = running_max + jnp.log(running_sum)
    merged = (
        attention.reshape(groups, rows, ratio, size)
        .transpose(1, 0, 2, 3)
        .reshape(rows, query_width)
        .astype(jnp.bfloat16)
    )
    residual = features + jnp.dot(merged, whole_output, preferred_element_type=jnp.float32)
    gain_second, whole_gate_up, whole_down = feedforward_params(
        feedforward_gain, gate_up, down_weight
    )
    inverse_two = rms_inverse(residual)
    normed_two = (residual * inverse_two * gain_second.astype(jnp.float32)).astype(jnp.bfloat16)
    gate_values = jnp.dot(normed_two, whole_gate_up, preferred_element_type=jnp.float32)
    gate = gate_values[:, :FF]
    upward = gate_values[:, FF:]
    sigmoid = jax.nn.sigmoid(gate)
    activation = (gate * sigmoid * upward).astype(jnp.bfloat16)
    outputs = (
        residual + jnp.dot(activation, whole_down, preferred_element_type=jnp.float32)
    ).astype(jnp.bfloat16)
    gain_second, whole_gate_up, whole_down = feedforward_params(
        feedforward_gain, gate_up, down_weight
    )
    tangent = cotangent[0]
    d_activation = contract_columns(tangent, whole_down)
    d_gate = d_activation * upward * sigmoid * (1.0 + gate * (1.0 - sigmoid))
    d_upward = d_activation * gate * sigmoid
    d_gate_up = jnp.concatenate([d_gate, d_upward], axis=1).astype(jnp.bfloat16)
    d_normed_two = contract_columns(d_gate_up, whole_gate_up)
    d_residual, grad_gain_two = norm_back(
        d_normed_two, residual, inverse_two, gain_second.astype(jnp.float32)
    )
    d_residual = d_residual + tangent.astype(jnp.float32)
    whole_gain, whole_projection, whole_bias, whole_output = attention_params(
        attention_gain, projection, projection_bias, output_weight
    )
    d_branch = d_residual.astype(jnp.bfloat16)
    d_merged = contract_columns(d_branch, whole_output).astype(jnp.bfloat16)
    d_attention = (
        d_merged.reshape(rows, groups, ratio, size)
        .transpose(1, 0, 2, 3)
        .reshape(groups, rows * ratio, size)
    )
    delta = jnp.sum(d_attention.astype(jnp.float32) * attention, axis=-1)
    zero_queries = jnp.zeros((groups, rows * ratio, size), jnp.float32)
    zero_pairs = jnp.zeros((rows, 2 * key_width), jnp.float32)
    d_queries, d_pairs = backward_update(
        zero_queries,
        zero_pairs,
        grouped,
        query_index,
        keys_values,
        own_index,
        d_attention,
        logsum,
        delta,
    )

    def backward_turn(turn, carry):
        d_queries, held, d_pairs = carry
        held = passed_along(held, "ctx", 1)
        d_pairs = send_back(d_pairs)
        source = (place - turn) % cycle
        d_queries, d_pairs = backward_update(
            d_queries,
            d_pairs,
            grouped,
            query_index,
            held,
            order_rows(block_order, source * rows, rows, half),
            d_attention,
            logsum,
            delta,
        )
        return (d_queries, held, d_pairs)

    d_queries, held, d_pairs = lax.fori_loop(
        1, cycle, backward_turn, (d_queries, keys_values, d_pairs)
    )
    d_pairs = send_back(d_pairs)
    d_query_heads = (
        d_queries.reshape(groups, rows, ratio, size)
        .transpose(1, 0, 2, 3)
        .reshape(rows, HEADS, size)
    )
    d_query_raw = rope_back(d_query_heads, cosine, sine)
    d_key_raw = rope_back(d_pairs[:, :key_width].reshape(rows, groups, size), cosine, sine)
    d_projected = jnp.concatenate(
        [
            d_query_raw.reshape(rows, query_width),
            d_key_raw.reshape(rows, key_width),
            d_pairs[:, key_width:],
        ],
        axis=1,
    ).astype(jnp.bfloat16)
    grad_bias = jnp.sum(d_projected.astype(jnp.float32), axis=0)
    d_normed_one = contract_columns(d_projected, whole_projection)
    d_features, grad_gain_one = norm_back(
        d_normed_one, features, inverse_one, whole_gain.astype(jnp.float32)
    )
    gradient = (d_residual + d_features).astype(jnp.bfloat16)
    rows_projection = owner_rows(normed_one, d_projected)
    rows_output = owner_rows(merged, d_branch)
    rows_gate_up = owner_rows(normed_two, d_gate_up)
    rows_down = owner_rows(activation, tangent)
    final_projection, final_output, final_gate_up, final_down = (
        lax.psum_scatter(
            rows_projection.astype(jnp.bfloat16), "ctx", scatter_dimension=1, tiled=True
        ).astype(jnp.float32),
        lax.psum_scatter(
            rows_output.astype(jnp.bfloat16), "ctx", scatter_dimension=1, tiled=True
        ).astype(jnp.float32),
        lax.psum_scatter(
            rows_gate_up.astype(jnp.bfloat16), "ctx", scatter_dimension=1, tiled=True
        ).astype(jnp.float32),
        lax.psum_scatter(
            rows_down.astype(jnp.bfloat16), "ctx", scatter_dimension=1, tiled=True
        ).astype(jnp.float32),
    )
    final_gain_one, final_bias, final_gain_two = (
        lax.psum_scatter(grad_gain_one, ("ctx", "fsdp"), scatter_dimension=0, tiled=True),
        lax.psum_scatter(grad_bias, ("ctx", "fsdp"), scatter_dimension=0, tiled=True),
        lax.psum_scatter(grad_gain_two, ("ctx", "fsdp"), scatter_dimension=0, tiled=True),
    )
    return (
        outputs[None],
        gradient[None],
        final_gain_one,
        final_projection,
        final_bias,
        final_output,
        final_gain_two,
        final_gate_up,
        final_down,
    )


def solution(mesh):
    return jax.shard_map(
        body,
        mesh=mesh,
        in_specs=(
            P("fsdp", "ctx", None),
            P("fsdp", "ctx"),
            P(),
            P("fsdp"),
            P("fsdp", None),
            P("fsdp"),
            P("fsdp", None),
            P("fsdp"),
            P("fsdp", None),
            P("fsdp", None),
            P("fsdp", "ctx", None),
        ),
        out_specs=(
            P("fsdp", "ctx", None),
            P("fsdp", "ctx", None),
            P(("ctx", "fsdp")),
            P("fsdp", "ctx"),
            P(("ctx", "fsdp")),
            P("fsdp", "ctx"),
            P(("ctx", "fsdp")),
            P("fsdp", "ctx"),
            P("fsdp", "ctx"),
        ),
        check_vma=False,
    )
```

profile of v0, /device:TPU:0, one launch (start us, length us, event | category | flops | bytes accessed | tf_op | source)
XLA Modules:
  0.0 2460.8 jit_solution(12207678242089483256)
XLA Ops:
  10.9 13.6 all-gather.2
  24.6 13.4 all-gather.1
  38.2 17.0 all-gather.3
  55.5 72.3 %all-gather.13.cloned.1.call-done = bf16[1536,2048]{1,0:T(8,128)(2,1)} async-done(((bf16[384,2048]{1,0:T(8,128)(2,1)}), bf16[1536,2048]{1,0:T(8,128)(2,1)}) %all-gather.13.cloned.1.call-update) | async-done | bytes 6291472 | tf_op jit(solution)/shard_map/all_gather | solution.py:136
  127.8 3.8 convolution_add_fusion.3
  137.8 46.1 %while.44 = (s32[]{:T(128)}, f32[2,768]{1,0:T(2,128)S(1)}, f32[2,768]{1,0:T(2,128)S(1)}, f32[2,768,128]{2,1,0:T(8,128)S(1)}, bf16[128,512]{0,1:T(8,128)(2,1)S(1)...) while((s32[]{:T(128)}, f32[2,768]{1,0:T(2,128)S(1)}, ...), condition=%wide.region_8.9_spmd.clone, body=%wide.region_4.8_spmd.clone.sunk | while | flops 102937232 | bytes 6012794 | solution.py:220
  139.1 4.1 collective-permute-done
  145.7 4.1 collective-permute-done
  152.2 4.1 collective-permute-done
  158.8 4.1 collective-permute-done
  165.4 4.1 collective-permute-done
  172.0 4.1 collective-permute-done
  178.6 4.1 collective-permute-done
  184.1 3.7 fusion.71
  188.9 28.2 %all-gather.15.cloned.1.call-done = bf16[1536,1536]{1,0:T(8,128)(2,1)} async-done(((bf16[384,1536]{1,0:T(8,128)(2,1)}), bf16[1536,1536]{1,0:T(8,128)(2,1)}) %all-gather.15.cloned.1.call-update) | async-done | bytes 4718608 | tf_op jit(solution)/shard_map/all_gather | solution.py:138
  220.6 911.1 %all-gather.17.cloned.1.call-done = bf16[1536,17920]{1,0:T(8,128)(2,1)} async-done(((bf16[384,17920]{1,0:T(8,128)(2,1)}), bf16[1536,17920]{1,0:T(8,128)(2,1)}) %all-gather.17.cloned.1.call-update) | async-done | bytes 55050256 | tf_op jit(solution)/shard_map/all_gather | solution.py:145
  1131.7 28.7 %fusion.75 = f32[128,17920]{1,0:T(8,128)} fusion(bf16[128,1536]{1,0:T(8,128)(2,1)S(1)} %multiply_convert_fusion.3, bf16[1536,17920]{1,0:T(8,128)(2,1)} %all-gather.17.cloned.1.call-done), kind=kOutput, calls=%fused_computation.181 | convolution fusion | flops 7046430720 | bytes 64618496 | tf_op jit(solution)/shard_map/dot_general | solution.py:236
  1160.4 434.6 %all-gather.19.cloned.1.call-done = bf16[8960,1536]{1,0:T(8,128)(2,1)} async-done(((bf16[2240,1536]{1,0:T(8,128)(2,1)}), bf16[8960,1536]{1,0:T(8,128)(2,1)}) %all-gather.19.cloned.1.call-update) | async-done | bytes 27525136 | tf_op jit(solution)/shard_map/all_gather | solution.py:146
  1595.1 18.5 multiply_convert_fusion.1
  1613.6 26.2 %multiply_reduce_fusion = (f32[1536]{0:T(1024)}, f32[128]{0:T(128)S(1)}, f32[128,1536]{1,0:T(8,128)}) fusion(f32[128,1536]{1,0:T(8,128)S(1)} %get-tuple-element.784, f32[128]{0:T(128)S(1)} %add_rsqrt_fusion, f32[1536]{0:T(1024)S(1)} %reshape.518, bf16[1536,17920]{1,0:T(8,128)(2,1)} %all-gather.17.cloned.1.call-done, ...), kind=kOutput, calls=%fused_computation.87 | convolution fusion | flops 7056783872 | bytes 61223936 | tf_op jit(solution)/shard_map/dot_general | solution.py:72
  1642.0 4.1 convolution_convert_fusion.4
  1657.8 64.5 %while.45 = (s32[]{:T(128)}, f32[2,768,128]{2,1,0:T(8,128)S(1)}, bf16[128,512]{0,1:T(8,128)(2,1)}, bf16[128,512]{0,1:T(8,128)(2,1)}, s32[]{:T(128)}, /*index=5*/...) while((s32[]{:T(128)}, f32[2,768,128]{2,1,0:T(8,128)S(1)}, ...), condition=%wide.region_14.15_spmd.clone, body=%wide.region_12.14_spmd.clone.sunk | while | flops 253830800 | bytes 9466070 | solution.py:300
  1668.3 4.3 collective-permute-done.1
  1676.8 4.9 collective-permute-done.1
  1686.0 4.9 collective-permute-done.1
  1695.2 4.9 collective-permute-done.1
  1704.5 4.9 collective-permute-done.1
  1713.7 4.9 collective-permute-done.1
  1735.9 4.7 pad_maximum_fusion
  1740.7 3.5 all-to-all-start.1
  1745.3 23.0 all-to-all-done.1
  1768.4 3.7 all-to-all-start
  1772.3 4.2 copy.219
  1776.5 14.5 all-to-all-done
  1791.0 4.5 all-to-all-start.3
  1795.6 3.5 convolution_convert_fusion.2
  1799.1 5.2 all-gather.21.cloned.1.call-done
  1804.3 3.8 convolution_convert_fusion.3
  1808.2 60.9 %all-to-all-done.3 = bf16[128,4,2240]{0,2,1:T(8,128)(2,1)} async-done(((bf16[128,4,2240]{0,2,1:T(8,128)(2,1)}), bf16[128,4,2240]{0,2,1:T(8,128)(2,1)}, u32[]{:S(2)}, u32[]{:S(2)}) %all-to-all-start.3) | async-done | bytes 2293792 | tf_op jit(solution)/shard_map/all_to_all | solution.py:151
  1869.1 4.2 copy.220
  1873.3 9.2 convolution_convert_fusion.1
  1883.6 29.7 %all_to_all.70 = bf16[128,4,384]{2,0,1:T(8,128)(2,1)S(1)} all-to-all(bf16[128,4,384]{2,0,1:T(8,128)(2,1)S(1)} %bitcast.243), channel_id=1, replica_groups=mesh['ctx'=8,'fsdp'=4] {'fsdp'}, dimensions={1} | all-to-all | bytes 786432 | tf_op jit(solution)/shard_map/all_to_all | solution.py:151
  1913.3 279.6 %all-gather.25.cloned.1.call-done = bf16[512,17920]{1,0:T(8,128)(2,1)} async-done(((bf16[128,17920]{1,0:T(8,128)(2,1)}), bf16[512,17920]{1,0:T(8,128)(2,1)}) %all-gather.25.cloned.1.call-update) | async-done | bytes 18350096 | tf_op jit(solution)/shard_map/all_gather | solution.py:152
  2192.9 16.1 convolution_convert_fusion
  2209.0 14.3 fusion.23
  2226.5 43.0 %all-reduce.3 = (f32[1536]{0:T(1024)S(1)}, f32[2048]{0:T(1024)S(1)}, f32[1536]{0:T(1024)S(1)}) all-reduce(f32[1536]{0:T(1024)S(1)} %get-tuple-element.705, f32[2048]{0:T(1024)S(1)} %get-tuple-element.752, f32[1536]{0:T(1024)S(1)} %copy-done.16), channel_id=3, replica_groups=mesh['ctx'=8,'fsdp'=4] {'ctx','fsdp'}, use_global_device_ids=true, to_apply=%region_17.18.clone | all-reduce | flops 5120 | bytes 40960
  2280.1 67.4 %reduce-scatter.11.cloned.1.call-done = bf16[2240,192]{0,1:T(8,128)(2,1)} async-done(((bf16[2240,1536]{0,1:T(8,128)(2,1)}), bf16[2240,192]{0,1:T(8,128)(2,1)}) %reduce-scatter.11.cloned.1.call-update) | async-done | bytes 860176 | tf_op jit(solution)/shard_map/reduce_scatter | solution.py:339
  2350.0 100.3 %reduce-scatter.9.cloned.1.call-done = bf16[384,2240]{0,1:T(8,128)(2,1)} async-done(((bf16[384,17920]{0,1:T(8,128)(2,1)}), bf16[384,2240]{0,1:T(8,128)(2,1)}) %reduce-scatter.9.cloned.1.call-update) | async-done | bytes 1720336 | tf_op jit(solution)/shard_map/reduce_scatter | solution.py:336
  (417 shorter events, 115.8 us)
Async XLA Ops:
  7.2 120.6 %all-gather.13.cloned.1.call-start = ((), (), s32[]{:S(2)}) async-start(), calls=%async_computation.8 | async-start | bytes 7864320 | tf_op jit(solution)/shard_map/all_gather | solution.py:136
  7.9 209.1 %all-gather.15.cloned.1.call-start = ((), (), s32[]{:S(2)}) async-start(), calls=%async_computation.9 | async-start | bytes 5898240 | tf_op jit(solution)/shard_map/all_gather | solution.py:138
  8.7 1123.0 %all-gather.17.cloned.1.call-start = ((), (), s32[]{:S(2)}) async-start(), calls=%async_computation.10 | async-start | bytes 68812800 | tf_op jit(solution)/shard_map/all_gather | solution.py:145
  9.4 15.2 copy-start.20
  9.4 28.7 %copy-start.21 = (bf16[384]{0:T(512)(128)(2,1)S(1)}, bf16[384]{0:T(512)(128)(2,1)}, u32[]{:S(2)}) copy-start(bf16[384]{0:T(512)(128)(2,1)} %param.22) | copy-start | bytes 2308
  9.4 45.8 %copy-start = (bf16[1,128,1536]{2,1,0:T(8,128)(2,1)S(1)}, bf16[1,128,1536]{2,1,0:T(8,128)(2,1)}, u32[]{:S(2)}) copy-start(bf16[1,128,1536]{2,1,0:T(8,128)(2,1)} %param.15) | copy-start | bytes 1179652
  9.5 1585.6 %all-gather.19.cloned.1.call-start = ((), (), s32[]{:S(2)}) async-start(), calls=%async_computation.11 | async-start | bytes 34406400 | tf_op jit(solution)/shard_map/all_gather | solution.py:146
  10.0 1785.5 %all-gather.23.cloned.1.call-start = ((), (), s32[]{:S(2)}) async-start(), calls=%async_computation.14 | async-start | bytes 1966080 | tf_op jit(solution)/shard_map/all_gather | solution.py:152
  10.8 122.0 %copy-start.7 = (f32[128,128]{0,1:T(8,128)}, f32[128,128]{0,1:T(8,128)S(1)}, u32[]{:S(2)}) copy-start(f32[128,128]{0,1:T(8,128)S(1)} %get-tuple-element.778) | copy-start | bytes 196612
  10.9 123.6 %copy-start.9 = (f32[128,128]{1,0:T(8,128)}, f32[128,128]{1,0:T(8,128)S(1)}, u32[]{:S(2)}) copy-start(f32[128,128]{1,0:T(8,128)S(1)} %copy.177) | copy-start | bytes 196612
  137.9 5.3 collective-permute-start
  144.4 5.3 collective-permute-start
  151.0 5.3 collective-permute-start
  157.6 5.3 collective-permute-start
  164.2 5.3 collective-permute-start
  170.8 5.3 collective-permute-start
  177.3 5.3 collective-permute-start
  220.4 1419.4 %copy-start.17 = (f32[128]{0:T(128)}, f32[128]{0:T(128)S(1)}, u32[]{:S(2)}) copy-start(f32[128]{0:T(128)S(1)} %add_rsqrt_fusion) | copy-start | bytes 1540
  220.5 1431.8 %copy-start.15 = (f32[2,768]{1,0:T(2,128)}, f32[2,768]{1,0:T(2,128)S(1)}, u32[]{:S(2)}) copy-start(f32[2,768]{1,0:T(2,128)S(1)} %log_add_fusion) | copy-start | bytes 18436
  220.6 939.8 %copy-start.3 = (bf16[128,1536]{1,0:T(8,128)(2,1)}, bf16[128,1536]{1,0:T(8,128)(2,1)S(1)}, u32[]{:S(2)}) copy-start(bf16[128,1536]{1,0:T(8,128)(2,1)S(1)} %multiply_convert_fusion.3) | copy-start | bytes 1179652
  220.6 1374.4 %copy-start.5 = (bf16[1,128,1536]{2,1,0:T(8,128)(2,1)S(1)}, bf16[1,128,1536]{2,1,0:T(8,128)(2,1)}, u32[]{:S(2)}) copy-start(bf16[1,128,1536]{2,1,0:T(8,128)(2,1)} %param.25) | copy-start | bytes 1179652
  1642.0 162.3 %all-gather.21.cloned.1.call-start = ((), (), s32[]{:S(2)}) async-start(), calls=%async_computation.12 | async-start | bytes 2621440 | tf_op jit(solution)/shard_map/all_gather | solution.py:152
  1657.8 5.5 collective-permute-start.1
  1657.9 8.5 collective-permute-start.2
  1667.1 5.5 collective-permute-start.1
  1667.1 8.5 collective-permute-start.2
  1676.3 5.5 collective-permute-start.1
  1676.3 8.5 collective-permute-start.2
  1685.5 5.5 collective-permute-start.1
  1685.5 8.5 collective-permute-start.2
  1694.7 5.5 collective-permute-start.1
  1694.7 8.5 collective-permute-start.2
  1703.9 5.5 collective-permute-start.1
  1703.9 8.5 collective-permute-start.2
  1713.1 5.5 collective-permute-start.1
  1713.1 8.5 collective-permute-start.2
  1726.1 5.5 collective-permute-start.3
  1735.1 138.2 %all-gather.27.cloned.1.call-start = ((), (), s32[]{:S(2)}) async-start(), calls=%async_computation.19 | async-start | bytes 1966080 | tf_op jit(solution)/shard_map/all_gather | solution.py:152
  1735.9 457.0 %all-gather.25.cloned.1.call-start = ((), (), s32[]{:S(2)}) async-start(), calls=%async_computation.16 | async-start | bytes 22937600 | tf_op jit(solution)/shard_map/all_gather | solution.py:152
  1740.7 27.7 %all-to-all-start.1 = ((bf16[128,4,384]{0,2,1:T(8,128)(2,1)}), bf16[128,4,384]{0,2,1:T(8,128)(2,1)S(1)}, u32[]{:S(2)}, u32[]{:S(2)}) async-start(bf16[128,4,384]{0,2,1:T(8,128)(2,1)} %bitcast.32), calls=%async_computation.2 | async-start | bytes 786432 | tf_op jit(solution)/shard_map/all_to_all | solution.py:151
  1768.4 22.6 all-to-all-start
  1791.0 78.1 %all-to-all-start.3 = ((bf16[128,4,2240]{0,2,1:T(8,128)(2,1)}), bf16[128,4,2240]{0,2,1:T(8,128)(2,1)}, u32[]{:S(2)}, u32[]{:S(2)}) async-start(bf16[128,4,2240]{0,2,1:T(8,128)(2,1)} %bitcast.221), calls=%async_computation.6 | async-start | bytes 4587520 | tf_op jit(solution)/shard_map/all_to_all | solution.py:151
  1795.5 478.4 %reduce-scatter.7.cloned.1.call-start = ((), (), s32[]{:S(2)}) async-start(), calls=%async_computation.15 | async-start | bytes 1327104 | tf_op jit(solution)/shard_map/reduce_scatter | solution.py:333
  1799.1 479.3 %reduce-scatter.5.cloned.1.call-start = ((), (), s32[]{:S(2)}) async-start(), calls=%async_computation.13 | async-start | bytes 1769472 | tf_op jit(solution)/shard_map/reduce_scatter | solution.py:330
  1808.1 539.4 %reduce-scatter.11.cloned.1.call-start = ((), (), s32[]{:S(2)}) async-start(), calls=%async_computation.18 | async-start | bytes 7962624 | tf_op jit(solution)/shard_map/reduce_scatter | solution.py:339
  1882.6 567.7 %reduce-scatter.9.cloned.1.call-start = ((), (), s32[]{:S(2)}) async-start(), calls=%async_computation.17 | async-start | bytes 15482880 | tf_op jit(solution)/shard_map/reduce_scatter | solution.py:336
  2209.0 14.3 slice-start
  2223.3 47.9 %copy-start.18 = (f32[128]{0:T(128)S(1)}, f32[128]{0:T(128)}, u32[]{:S(2)}) copy-start(f32[128]{0:T(128)} %copy-done.17) | copy-start | bytes 1540
  (23 other events, 131.6 us)
Sparse Core Ops, SparseCore 0:
  9.6 118.2 all-gather.12
  129.4 87.6 all-gather.14
  218.7 913.0 all-gather.16
  1133.1 461.8 all-gather.18
  1642.1 35.2 all-gather.22
  1735.3 69.0 all-gather.20
  1805.9 57.7 all-gather.26
  1865.3 327.5 all-gather.24
  2196.1 39.6 reduce-scatter.6
  2239.5 38.8 reduce-scatter.4
  2281.9 65.4 reduce-scatter.10
  2350.8 99.3 reduce-scatter.8
where the time goes:
time: 2470 us; the launch traced here: 2460 us
  waiting for transfers between devices  2070 us (84%)
  matrix products  163 us (7%)
  blocking collectives  117 us (5%)
  other arithmetic  48.9 us (2%)
  local copies, waits for them, and re-layouts  33.7 us (1%)
    all_gather x1, waiting for transfers between devices, feedforward_params(): lax.all_gather(gate_up, 'fsdp', axis=0, tiled=True)  911 us
    all_gather x1, waiting for transfers between devices, feedforward_params(): lax.all_gather(down_weight, 'fsdp', axis=0, tiled=True)  435 us
    all_gather x4, waiting for transfers between devices, owner_rows(): lax.all_gather(right, 'fsdp', axis=0, tiled=True)  285 us
    reduce_scatter x1, waiting for transfers between devices, body(): lax.psum_scatter(rows_gate_up.astype(jnp.bfloat16), 'ctx', scatter_dimens...  100 us
    all_to_all x3, waiting for transfers between devices, owner_rows(): lax.all_to_all(left, 'fsdp', split_axis=1, concat_axis=0, tiled=True)  98.5 us
    all_gather x1, waiting for transfers between devices, attention_params(): lax.all_gather(projection, 'fsdp', axis=0, tiled=True)  72.3 us
    reduce_scatter x1, waiting for transfers between devices, body(): lax.psum_scatter(rows_down.astype(jnp.bfloat16), 'ctx', scatter_dimension...  67.4 us
    ppermute x22, waiting for transfers between devices, passed_along(): return lax.ppermute(block, axis, route)  63.6 us
  transfers between devices with their start and end apart: 37, of which 27 were waited for; matrix products, arithmetic and copies ran while one was open for 8% of the time, Pallas kernels for 0%

commit v1 on v0

v1 whole, which is shorter than its diff:
```python
import math

import jax
import jax.numpy as jnp
from jax import lax
from jax.sharding import PartitionSpec as P

HEADS = 12
KV_HEADS = 2
HEAD = 128
FF = 8960
GROUP = 2

EPS = 1e-06
THETA = 1000000.0
NEGATIVE = -1e30
BF = jnp.bfloat16
F32 = jnp.float32


def rope_tables(places):
    freq = THETA ** (-jnp.arange(0, HEAD, 2).astype(F32) / HEAD)
    angle = places.astype(F32)[:, None] * freq[None, :]
    angle = jnp.concatenate([angle, angle], axis=-1)
    return (jnp.cos(angle), jnp.sin(angle))


def rotate(values):
    middle = values.shape[-1] // 2
    return jnp.concatenate([-values[..., middle:], values[..., :middle]], axis=-1)


def apply_rope(values, cosine, sine):
    return values * cosine[:, None, :] + rotate(values) * sine[:, None, :]


def rope_back(grads, cosine, sine):
    return grads * cosine[:, None, :] - rotate(grads * sine[:, None, :])


def order_rows(block_order, start, count, half):
    offsets = start + jnp.arange(count, dtype=jnp.int32)
    slots = offsets // half
    table = jnp.arange(block_order.shape[0], dtype=jnp.int32)
    picked = jnp.sum(jnp.where(slots[:, None] == table[None, :], block_order[None, :], 0), axis=1)
    return picked * half + offsets % half


def rms_inverse(values):
    return lax.rsqrt(jnp.mean(values * values, axis=-1, keepdims=True) + EPS)


def norm_back(d_normed, values, inverse, gain):
    unit = values * inverse
    d_unit = d_normed * gain
    d_gain = jnp.sum(d_normed * unit, axis=0)
    d_values = inverse * (d_unit - unit * jnp.mean(d_unit * unit, axis=-1, keepdims=True))
    return (d_values, d_gain)


def dot(left, right, dims, out=F32):
    return lax.dot_general(left, right, (dims, ((), ())), preferred_element_type=out)


def swapped(x, size):
    return lax.ppermute(x, "fsdp", [(i, i ^ 1) for i in range(size)])


def gather_tokens(x, size):
    both = jnp.stack([x, swapped(x, size)])
    return lax.all_gather(both, "ctx", axis=1, tiled=True)


def scatter_tokens(partial, size):
    parts = lax.psum_scatter(partial, "ctx", scatter_dimension=1, tiled=True)
    return parts[0].astype(F32) + swapped(parts[1], size).astype(F32)


def body(
    inputs,
    positions,
    block_order,
    attention_gain,
    projection,
    projection_bias,
    output_weight,
    feedforward_gain,
    gate_up,
    down_weight,
    cotangent,
):
    rows, width = inputs.shape[1:]
    half = rows // 2
    ratio = HEADS // KV_HEADS
    query_width = HEADS * HEAD
    key_width = KV_HEADS * HEAD
    cycle = lax.axis_size("ctx")
    owners = lax.axis_size("fsdp")
    place = lax.axis_index("ctx")
    owner = lax.axis_index("fsdp")
    fold = owners // GROUP
    unit = FF // (owners * cycle)
    depth = width // owners
    length = rows * cycle

    slab = depth // cycle
    whole_projection = lax.all_gather(
        lax.dynamic_slice_in_dim(projection, place * slab, slab, 0), ("fsdp", "ctx"), axis=0, tiled=True
    )
    whole_output = lax.all_gather(
        lax.dynamic_slice_in_dim(output_weight, place * slab, slab, 0), ("fsdp", "ctx"), axis=0, tiled=True
    )
    small = lax.all_gather(
        jnp.concatenate([attention_gain, feedforward_gain, projection_bias]), "fsdp", axis=0
    )
    gain_one = small[:, :depth].reshape(-1).astype(F32)
    gain_two = small[:, depth : 2 * depth].reshape(-1).astype(F32)
    bias = small[:, 2 * depth :].reshape(-1).astype(F32)

    pieces = []
    for side in range(2):
        for plane in range(owners):
            start = side * FF + plane * (FF // owners) + place * unit
            pieces.append(lax.dynamic_slice_in_dim(gate_up, start, unit, 1))

    def part(side, to):
        return jnp.concatenate(
            [pieces[side * owners + (to + GROUP * b) % owners] for b in range(fold)], axis=1
        )

    sent = jnp.stack([jnp.stack([part(side, to) for side in range(2)]) for to in range(owners)])
    got = lax.all_to_all(sent, "fsdp", split_axis=0, concat_axis=0, tiled=True)
    gate_weight = got[:, 0].reshape(width, fold * unit)
    up_weight = got[:, 1].reshape(width, fold * unit)
    own_down = lax.dynamic_slice_in_dim(down_weight, place * unit, unit, 0)
    down = [own_down]
    for b in range(1, fold):
        route = [((i + GROUP * b) % owners, i) for i in range(owners)]
        down.append(lax.ppermute(own_down, "fsdp", route))
    down = jnp.concatenate(down, axis=0)

    tangent = cotangent[0]
    tangents = gather_tokens(tangent, owners).reshape(GROUP * length, width)

    features = inputs[0].astype(F32)
    inverse_one = rms_inverse(features)
    normed_one = (features * inverse_one * gain_one).astype(BF)
    projected = dot(normed_one, whole_projection, ((1,), (0,))) + bias
    cosine, sine = rope_tables(positions[0])
    queries = apply_rope(projected[:, :query_width].reshape(rows, HEADS, HEAD), cosine, sine).astype(BF)
    keys = apply_rope(
        projected[:, query_width : query_width + key_width].reshape(rows, KV_HEADS, HEAD), cosine, sine
    ).astype(BF)
    values = projected[:, query_width + key_width :].astype(BF)
    pairs = lax.all_gather(
        jnp.concatenate([keys.reshape(rows, key_width), values], axis=1), "ctx", axis=0, tiled=True
    )
    all_keys = pairs[:, :key_width].reshape(length, KV_HEADS, HEAD)
    all_values = pairs[:, key_width:].reshape(length, KV_HEADS, HEAD)
    grouped = queries.reshape(rows, KV_HEADS, ratio, HEAD).transpose(1, 2, 0, 3)
    own_index = order_rows(block_order, place * rows, rows, half)
    all_index = order_rows(block_order, 0, length, half)
    mask = (all_index[None, :] <= own_index[:, None])[None, None]
    scale = 1.0 / math.sqrt(HEAD)

    def weights_of():
        scores = jnp.einsum("grqd,kgd->grqk", grouped, all_keys, preferred_element_type=F32) * scale
        return jnp.where(mask, scores, NEGATIVE)

    scores = weights_of()
    top = jnp.max(scores, axis=-1, keepdims=True)
    probs = jnp.exp(scores - top)
    total = jnp.sum(probs, axis=-1, keepdims=True)
    probs = probs / total
    low_probs = probs.astype(BF)
    attention = jnp.einsum("grqk,kgd->grqd", low_probs, all_values, preferred_element_type=F32)
    merged = attention.transpose(2, 0, 1, 3).reshape(rows, query_width).astype(BF)
    residual = features + dot(merged, whole_output, ((1,), (0,)))
    inverse_two = rms_inverse(residual)
    normed_two = (residual * inverse_two * gain_two).astype(BF)

    tokens = gather_tokens(normed_two, owners).reshape(GROUP * length, width)
    gate = dot(tokens, gate_weight, ((1,), (0,)))
    upward = dot(tokens, up_weight, ((1,), (0,)))
    sigmoid = jax.nn.sigmoid(gate)
    activation = (gate * sigmoid * upward).astype(BF)
    branch = dot(activation, down, ((1,), (0,)), BF).reshape(GROUP, length, width)
    outputs = (residual + scatter_tokens(branch, owners)).astype(BF)
    d_activation = dot(tangents, down, ((1,), (1,)))
    d_gate = (d_activation * upward * sigmoid * (1.0 + gate * (1.0 - sigmoid))).astype(BF)
    d_upward = (d_activation * gate * sigmoid).astype(BF)
    d_tokens = (
        dot(d_gate, gate_weight, ((1,), (1,))) + dot(d_upward, up_weight, ((1,), (1,)))
    ).astype(BF)
    d_normed_two = scatter_tokens(d_tokens.reshape(GROUP, length, width), owners)
    grad_gate = dot(tokens, d_gate, ((0,), (0,)), BF)
    grad_up = dot(tokens, d_upward, ((0,), (0,)), BF)
    grad_down = dot(activation, tangents, ((0,), (0,)), BF)

    mine = lax.all_to_all(
        jnp.stack([grad_gate.reshape(owners, depth, -1), grad_up.reshape(owners, depth, -1)], 1),
        "fsdp", split_axis=0, concat_axis=0, tiled=True,
    )
    folded = []
    for plane in range(owners):
        total_piece = 0.0
        for source in range(plane % GROUP, owners, GROUP):
            b = ((plane - source) // GROUP) % fold
            total_piece = total_piece + mine[source, :, :, b * unit : (b + 1) * unit].astype(F32)
        folded.append(total_piece.astype(BF))
    folded = jnp.stack(folded, axis=1)
    spread = lax.all_to_all(
        folded.reshape(cycle, 2 * owners // cycle, depth, unit), "ctx", split_axis=0, concat_axis=0, tiled=True
    )
    final_gate_up = spread.transpose(2, 1, 0, 3).reshape(depth, -1).astype(F32)
    grad_down = grad_down.reshape(fold, unit, width)
    total_down = grad_down[0].astype(F32)
    for b in range(1, fold):
        route = [(i, (i + GROUP * b) % owners) for i in range(owners)]
        total_down = total_down + lax.ppermute(grad_down[b], "fsdp", route).astype(F32)
    final_down = lax.all_to_all(
        total_down.astype(BF).reshape(unit, cycle, width // cycle).transpose(1, 0, 2),
        "ctx", split_axis=0, concat_axis=0, tiled=True,
    ).reshape(-1, width // cycle).astype(F32)

    d_residual, grad_gain_two = norm_back(d_normed_two, residual, inverse_two, gain_two)
    d_residual = d_residual + tangent.astype(F32)
    d_branch = d_residual.astype(BF)
    d_merged = dot(d_branch, whole_output, ((1,), (1,))).astype(BF)
    d_attention = d_merged.reshape(rows, KV_HEADS, ratio, HEAD).transpose(1, 2, 0, 3)
    delta = jnp.sum(d_attention.astype(F32) * attention, axis=-1, keepdims=True)
    d_values = jnp.einsum("grqk,grqd->kgd", low_probs, d_attention, preferred_element_type=F32)
    d_probs = jnp.einsum("grqd,kgd->grqk", d_attention, all_values, preferred_element_type=F32)
    d_scores = (probs * (d_probs - delta)).astype(BF)
    d_queries = jnp.einsum("grqk,kgd->qgrd", d_scores, all_keys, preferred_element_type=F32) * scale
    d_keys = jnp.einsum("grqk,grqd->kgd", d_scores, grouped, preferred_element_type=F32) * scale
    d_pairs = jnp.concatenate(
        [d_keys.reshape(length, key_width), d_values.reshape(length, key_width)], axis=1
    ).astype(BF)
    d_pairs = lax.psum_scatter(d_pairs, "ctx", scatter_dimension=0, tiled=True).astype(F32)
    d_query_raw = rope_back(d_queries.reshape(rows, HEADS, HEAD), cosine, sine)
    d_key_raw = rope_back(d_pairs[:, :key_width].reshape(rows, KV_HEADS, HEAD), cosine, sine)
    d_projected = jnp.concatenate(
        [d_query_raw.reshape(rows, query_width), d_key_raw.reshape(rows, key_width), d_pairs[:, key_width:]],
        axis=1,
    ).astype(BF)
    grad_bias = jnp.sum(d_projected.astype(F32), axis=0)
    d_normed_one = dot(d_projected, whole_projection, ((1,), (1,)))
    d_features, grad_gain_one = norm_back(d_normed_one, features, inverse_one, gain_one)
    gradient = (d_residual + d_features).astype(BF)

    def columns_home(left, right):
        whole_left = lax.all_gather(left, "ctx", axis=0, tiled=True)
        share = right.shape[1] // cycle
        sliced = lax.all_to_all(
            right.reshape(rows, cycle, share).transpose(1, 0, 2), "ctx", split_axis=0, concat_axis=0, tiled=True
        ).reshape(length, share)
        partial = dot(whole_left, sliced, ((0,), (0,)), BF).reshape(owners, depth, share)
        parts = lax.all_to_all(partial, "fsdp", split_axis=0, concat_axis=0, tiled=True)
        return jnp.sum(parts.astype(F32), axis=0)

    final_output = columns_home(merged, d_branch)
    final_projection = columns_home(normed_one, d_projected)
    count = owners * cycle
    sums = jnp.concatenate(
        [grad_gain_one.reshape(count, -1), grad_bias.reshape(count, -1), grad_gain_two.reshape(count, -1)], axis=1
    )
    sums = lax.psum_scatter(sums, ("ctx", "fsdp"), scatter_dimension=0, tiled=True)[0]
    first = width // count
    last = sums.shape[0] - first
    return (
        outputs[None],
        gradient[None],
        sums[:first],
        final_projection,
        sums[first:last],
        final_output,
        sums[last:],
        final_gate_up,
        final_down,
    )


def solution(mesh):
    return jax.shard_map(
        body,
        mesh=mesh,
        in_specs=(
            P("fsdp", "ctx", None),
            P("fsdp", "ctx"),
            P(),
            P("fsdp"),
            P("fsdp", None),
            P("fsdp"),
            P("fsdp", None),
            P("fsdp"),
            P("fsdp", None),
            P("fsdp", None),
            P("fsdp", "ctx", None),
        ),
        out_specs=(
            P("fsdp", "ctx", None),
            P("fsdp", "ctx", None),
            P(("ctx", "fsdp")),
            P("fsdp", "ctx"),
            P(("ctx", "fsdp")),
            P("fsdp", "ctx"),
            P(("ctx", "fsdp")),
            P("fsdp", "ctx"),
            P("fsdp", "ctx"),
        ),
        check_vma=False,
    )
```

time: 2470 us -> 774 us (0.31)
  waiting for transfers between devices: 2070 us -> 432 us
  blocking collectives: 117 us -> 54.8 us
  matrix products: 163 us -> 113 us
  local copies, waits for them, and re-layouts: 33.7 us -> 66.2 us
  starting transfers between devices: 14.9 us -> 45.1 us
    all_gather x8 -> x7, waiting for transfers between devices: 1730 us -> 128 us  [the longest x1 54.7 us: body(): lax.all_gather(lax.dynamic_slice_in_dim(projection, place * slab, slab, 0...]
    reduce_scatter x4 -> x3, waiting for transfers between devices: 170 us -> 50.9 us  [the longest x2 50.9 us: scatter_tokens(): parts = lax.psum_scatter(partial, 'ctx', scatter_dimension=1, tiled=True)]
    dot_general x67 -> x20, matrix products: 163 us -> 108 us  [the longest x15 96.1 us: dot(): lax.dot_general(left, right, (dims, ((), ())), preferred_element_type=out)]
    ppermute x22 -> x6, waiting for transfers between devices: 63.6 us -> 113 us  [the longest x1 93 us: body(): lax.ppermute(grad_down[b], 'fsdp', route).astype(F32)]
    all_to_all x3 -> x8, waiting for transfers between devices: 98.5 us -> 139 us  [the longest x1 91.3 us: body(): got = lax.all_to_all(sent, 'fsdp', split_axis=0, concat_axis=0, tiled=True)]
    all_to_all x1 -> x0, blocking collectives: 29.7 us -> none  [owner_rows(): lax.all_to_all(left, 'fsdp', split_axis=1, concat_axis=0, tiled=True)]
    all_gather x3 -> x1, blocking collectives: 44.1 us -> 14.9 us  [body(): lax.all_gather(jnp.concatenate([attention_gain, feedforward_gain, project...]
  transfers between devices with their start and end apart: 37 -> 24, of which waited for: 27 -> 14; matrix products, arithmetic and copies ran while one was open for 8% -> 23% of each run, Pallas kernels for 0% -> 0%
where the time goes in v1:
time: 774 us; the launch traced here: 765 us
  waiting for transfers between devices  432 us (56%)
  matrix products  113 us (15%)
  local copies, waits for them, and re-layouts  66.2 us (9%)
  blocking collectives  54.8 us (7%)
  starting transfers between devices  45.1 us (6%)
  other arithmetic  37.7 us (5%)
  between operations  15.7 us (2%)
    dot_general x15, matrix products, dot(): lax.dot_general(left, right, (dims, ((), ())), preferred_element_type=out)  96.1 us
    ppermute x1, waiting for transfers between devices, body(): lax.ppermute(grad_down[b], 'fsdp', route).astype(F32)  93 us
    all_to_all x1, waiting for transfers between devices, body(): got = lax.all_to_all(sent, 'fsdp', split_axis=0, concat_axis=0, tiled=True)  91.3 us
    all_gather x1, waiting for transfers between devices, body(): lax.all_gather(lax.dynamic_slice_in_dim(projection, place * slab, slab, 0...  54.7 us
    all_gather x1, waiting for transfers between devices, body(): lax.all_gather(lax.dynamic_slice_in_dim(output_weight, place * slab, slab...  53.9 us
    reduce_scatter x2, waiting for transfers between devices, scatter_tokens(): parts = lax.psum_scatter(partial, 'ctx', scatter_dimension=1, tiled=True)  50.9 us
    unnamed x1, blocking collectives  39.9 us
    ppermute x4, waiting for transfers between devices, swapped(): return lax.ppermute(x, 'fsdp', [(i, i ^ 1) for i in range(size)])  19.5 us
  transfers between devices with their start and end apart: 24, of which 14 were waited for; matrix products, arithmetic and copies ran while one was open for 23% of the time, Pallas kernels for 0%

profile of v1, /device:TPU:0, one launch (start us, length us, event | category | flops | bytes accessed | tf_op | source)
XLA Modules:
  0.0 765.0 jit_solution(17226624631359661983)
XLA Ops:
  10.1 14.9 %all-gather.1 = bf16[4,1,1280]{2,1,0:T(2,128)(2,1)S(1)} all-gather(bf16[1,1,1280]{2,1,0:T(2,128)(2,1)S(1)} %reshape.500), channel_id=2, replica_groups=mesh['ctx'=8,'fsdp'=4] {'fsdp'}, dimensions={0}, use_global_device_ids=true | all-gather | bytes 12800 | tf_op jit(solution)/shard_map/all_gather | solution.py:113
  28.6 54.7 %all-gather.10.cloned.1.call-done = bf16[1536,2048]{1,0:T(8,128)(2,1)} async-done(((bf16[48,2048]{1,0:T(8,128)(2,1)}), bf16[1536,2048]{1,0:T(8,128)(2,1)}) %all-gather.10.cloned.1.call-update) | async-done | bytes 6291472 | tf_op jit(solution)/shard_map/all_gather | solution.py:107
  83.3 3.8 convolution_add_fusion.1
  91.2 19.4 %all-gather.12.cloned.1.call-done = bf16[1024,512]{1,0:T(8,128)(2,1)} async-done(((bf16[128,512]{1,0:T(8,128)(2,1)}), bf16[1024,512]{1,0:T(8,128)(2,1)}) %all-gather.12.cloned.1.call-update) | async-done | bytes 1048592 | tf_op jit(solution)/shard_map/all_gather | solution.py:155
  112.5 4.8 fusion.70
  117.4 3.5 fusion.5
  123.7 53.9 %all-gather.14.cloned.1.call-done = bf16[1536,1536]{1,0:T(8,128)(2,1)} async-done(((bf16[48,1536]{1,0:T(8,128)(2,1)}), bf16[1536,1536]{1,0:T(8,128)(2,1)}) %all-gather.14.cloned.1.call-update) | async-done | bytes 4718608 | tf_op jit(solution)/shard_map/all_gather | solution.py:110
  177.7 3.2 multiply_reduce_fusion.3
  182.7 9.7 %collective-permute-done = bf16[128,1536]{1,0:T(8,128)(2,1)S(1)} collective-permute-done((bf16[128,1536]{1,0:T(8,128)(2,1)S(1)}, bf16[128,1536]{1,0:T(8,128)(2,1)S(1)}, u32[]{:S(2)}, u32[]{:S(2)}) %collective-permute-start) | collective-permute-done | bytes 393248 | tf_op jit(solution)/shard_map/ppermute | solution.py:66
  195.1 9.0 %collective-permute-done.3 = bf16[128,1536]{1,0:T(8,128)(2,1)S(1)} collective-permute-done((bf16[128,1536]{1,0:T(8,128)(2,1)S(1)}, bf16[128,1536]{1,0:T(8,128)(2,1)S(1)}, u32[]{:S(2)}, u32[]{:S(2)}) %collective-permute-start.3) | collective-permute-done | bytes 393248 | tf_op jit(solution)/shard_map/ppermute | solution.py:66
  205.1 4.2 constant_dynamic-slice_fusion.5
  224.6 4.7 all-to-all-start
  233.5 91.3 %all-to-all-done = bf16[4,2,384,560]{2,3,1,0:T(8,128)(2,1)} async-done(((bf16[4,2,384,560]{2,3,1,0:T(8,128)(2,1)}), bf16[4,2,384,560]{2,3,1,0:T(8,128)(2,1)}, u32[]{:S(2)}, u32[]{:S(2)}) %all-to-all-start) | async-done | bytes 3440672 | tf_op jit(solution)/shard_map/all_to_all | solution.py:132
  331.4 9.2 %fusion.73 = f32[2048,560]{0,1:T(8,128)} fusion(bf16[2048,1536]{1,0:T(8,128)(2,1)} %bitcast.252, bf16[1536,560]{0,1:T(8,128)(2,1)} %bitcast.274), kind=kOutput, calls=%fused_computation.187 | convolution fusion | flops 3523215360 | bytes 12599296 | tf_op jit(solution)/shard_map/dot_general | solution.py:62
  340.6 5.8 fusion.72
  346.4 10.8 %multiply_convert_fusion.1 = (bf16[2048,560]{0,1:T(8,128)(2,1)S(1)}, bf16[2048,560]{0,1:T(8,128)(2,1)S(1)}, bf16[2048,560]{0,1:T(8,128)(2,1)}) fusion(f32[2048,560]{0,1:T(8,128)} %fusion.72, f32[2048,560]{0,1:T(8,128)} %fusion.73, bf16[2048,1536]{1,0:T(8,128)(2,1)} %bitcast.290, bf16[280,1536]{1,0:T(8,128)(2,1)} %collective-permute-done.1, ...), kind=kOutput, calls=%fused_computation.6 | convolution fusion | flops 3545006080 | bytes 24068096 | tf_op jit(solution)/shard_map/dot_general | solution.py:62
  357.2 5.1 fusion.74
  362.4 7.0 add_convert_fusion
  371.0 8.9 %copy.168 = bf16[1536,2048]{1,0:T(8,128)(2,1)} copy(bf16[1536,2048]{0,1:T(8,128)(2,1)} %bitcast.253) | data formatting | bytes 12582912 | tf_op jit(solution)/shard_map/dot_general | solution.py:62
  379.9 50.9 %reduce-scatter.6.cloned.1.call-done = bf16[2,128,1536]{2,1,0:T(8,128)(2,1)} async-done(((bf16[2,1024,1536]{2,1,0:T(8,128)(2,1)}), bf16[2,128,1536]{2,1,0:T(8,128)(2,1)}) %reduce-scatter.6.cloned.1.call-update) | async-done | bytes 786448 | tf_op jit(solution)/shard_map/reduce_scatter | solution.py:75
  433.4 8.5 %fusion.10 = bf16[4,1,384,560]{2,3,0,1:T(8,128)(2,1)} fusion(bf16[4,384,2048]{2,1,0:T(8,128)(2,1)} %bitcast.256, bf16[2048,560]{0,1:T(8,128)(2,1)} %copy-done.46), kind=kOutput, calls=%fused_computation.28 | convolution fusion | flops 3523215360 | bytes 10305536 | tf_op jit(solution)/shard_map/dot_general | solution.py:62
  443.3 4.7 convolution_convert_fusion
  449.3 3.9 multiply_convert_fusion
  455.7 3.3 fusion.18
  461.3 7.5 fusion.13
  471.3 4.9 all-to-all-start.5
  476.3 9.2 %fusion.24 = bf16[2048,1536]{1,0:T(8,128)(2,1)} fusion(bf16[2048,560]{0,1:T(8,128)(2,1)} %get-tuple-element.25, bf16[280,1536]{1,0:T(8,128)(2,1)} %collective-permute-done.1, bf16[280,1536]{1,0:T(8,128)(2,1)S(1)} %copy-done.31), kind=kOutput, calls=%fused_computation.46 | convolution fusion | flops 3526656000 | bytes 10305536 | tf_op jit(solution)/shard_map/dot_general | solution.py:62
  485.5 7.7 %fusion.77 = bf16[560,1536]{1,0:T(8,128)(2,1)S(1)} fusion(bf16[2048,560]{0,1:T(8,128)(2,1)} %get-tuple-element.25, bf16[2048,1536]{1,0:T(8,128)(2,1)} %bitcast.291), kind=kOutput, calls=%fused_computation.191 | convolution fusion | flops 3523215360 | bytes 10305536 | tf_op jit(solution)/shard_map/dot_general | solution.py:62
  496.1 93.0 %collective-permute-done.5 = bf16[280,1536]{1,0:T(8,128)(2,1)S(1)} collective-permute-done((bf16[280,1536]{1,0:T(8,128)(2,1)S(1)}, bf16[280,1536]{1,0:T(8,128)(2,1)S(1)}, u32[]{:S(2)}, u32[]{:S(2)}) %collective-permute-start.5) | collective-permute-done | bytes 860192 | tf_op jit(solution)/shard_map/ppermute | solution.py:220
  593.5 3.6 all-to-all-start.7
  601.0 14.5 %all-to-all-done.7 = bf16[8,280,192]{2,1,0:T(8,128)(2,1)S(1)} async-done(((bf16[8,280,192]{2,1,0:T(8,128)(2,1)}), bf16[8,280,192]{2,1,0:T(8,128)(2,1)S(1)}, u32[]{:S(2)}, u32[]{:S(2)}) %all-to-all-start.7) | async-done | bytes 860192 | tf_op jit(solution)/shard_map/all_to_all | solution.py:221
  615.5 4.3 all-to-all-start.6
  619.8 4.7 copy.190
  629.0 13.4 %all-to-all-done.6 = bf16[8,1,384,280]{2,3,1,0:T(8,128)(2,1)} async-done(((bf16[8,1,384,280]{2,3,1,0:T(8,128)(2,1)}), bf16[8,1,384,280]{2,3,1,0:T(8,128)(2,1)}, u32[]{:S(2)}, u32[]{:S(2)}) %all-to-all-start.6) | async-done | bytes 1720352 | tf_op jit(solution)/shard_map/all_to_all | solution.py:212
  642.4 3.4 convert_element_type.389
  646.7 4.1 all-to-all-start.3
  650.9 3.1 convolution_multiply_fusion
  655.6 3.6 all-to-all-done.3
  660.6 3.9 fusion.76
  664.6 4.9 all-to-all-start.4
  674.3 9.8 %all-to-all-done.4 = bf16[4,384,192]{1,2,0:T(8,128)(2,1)S(1)} async-done(((bf16[4,384,192]{1,2,0:T(8,128)(2,1)}), bf16[4,384,192]{1,2,0:T(8,128)(2,1)S(1)}, u32[]{:S(2)}, u32[]{:S(2)}) %all-to-all-start.4) | async-done | bytes 589856 | tf_op jit(solution)/shard_map/all_to_all | solution.py:259
  684.1 3.5 all-to-all-start.1
  690.3 7.0 all-to-all-done.1
  697.3 3.8 fusion.75
  701.0 4.2 all-to-all-start.2
  705.3 6.0 fusion.31
  711.6 39.9 %all-reduce = f32[32,160]{1,0:T(8,128)S(1)} all-reduce(f32[32,160]{1,0:T(8,128)S(1)} %pad_maximum_fusion.13), channel_id=6, replica_groups=mesh['ctx'=8,'fsdp'=4] {'ctx','fsdp'}, use_global_device_ids=true, to_apply=%region_15.16.clone | all-reduce | flops 5120 | bytes 40960
  752.6 3.1 fusion.50
  (251 shorter events, 91.1 us)
Async XLA Ops:
  7.2 76.1 %all-gather.10.cloned.1.call-start = ((), (), s32[]{:S(2)}) async-start(), calls=%async_computation.11 | async-start | bytes 6488064 | tf_op jit(solution)/shard_map/all_gather | solution.py:107
  9.3 101.2 %all-gather.12.cloned.1.call-start = ((), (), s32[]{:S(2)}) async-start(), calls=%async_computation.12 | async-start | bytes 1179648 | tf_op jit(solution)/shard_map/all_gather | solution.py:155
  25.0 58.3 %copy-start.34 = (f32[1536]{0:T(1024)}, f32[1536]{0:T(1024)S(1)}, u32[]{:S(2)}) copy-start(f32[1536]{0:T(1024)S(1)} %reshape.492) | copy-start | bytes 18436
  26.1 65.0 %copy-start.23 = (f32[128,128]{0,1:T(8,128)}, f32[128,128]{0,1:T(8,128)S(1)}, u32[]{:S(2)}) copy-start(f32[128,128]{0,1:T(8,128)S(1)} %get-tuple-element.54) | copy-start | bytes 196612
  26.1 64.9 %copy-start.25 = (f32[128,128]{0,1:T(8,128)}, f32[128,128]{0,1:T(8,128)S(1)}, u32[]{:S(2)}) copy-start(f32[128,128]{0,1:T(8,128)S(1)} %get-tuple-element.55) | copy-start | bytes 196612
  26.2 61.3 %copy-start.32 = (f32[128,128]{1,0:T(8,128)}, f32[128,128]{1,0:T(8,128)S(1)}, u32[]{:S(2)}) copy-start(f32[128,128]{1,0:T(8,128)S(1)} %copy.142) | copy-start | bytes 196612
  27.5 55.9 %copy-start.41 = (f32[128]{0:T(128)}, f32[128]{0:T(128)S(1)}, u32[]{:S(2)}) copy-start(f32[128]{0:T(128)S(1)} %add_rsqrt_fusion.1) | copy-start | bytes 1540
  28.6 58.5 %copy-start.6 = (bf16[128,1536]{1,0:T(8,128)(2,1)}, bf16[128,1536]{1,0:T(8,128)(2,1)S(1)}, u32[]{:S(2)}) copy-start(bf16[128,1536]{1,0:T(8,128)(2,1)S(1)} %fusion.25) | copy-start | bytes 1179652
  88.5 89.2 %all-gather.14.cloned.1.call-start = ((), (), s32[]{:S(2)}) async-start(), calls=%async_computation.13 | async-start | bytes 4866048 | tf_op jit(solution)/shard_map/all_gather | solution.py:110
  90.1 241.3 %all-gather.16.cloned.1.call-start = ((), (), s32[]{:S(2)}) async-start(), calls=%async_computation.14 | async-start | bytes 7077888 | tf_op jit(solution)/shard_map/all_gather | solution.py:71
  91.2 26.2 %copy-start.19 = (bf16[2,6,128,128]{2,3,1,0:T(8,128)(2,1)}, bf16[2,6,128,128]{2,3,1,0:T(8,128)(2,1)S(1)}, u32[]{:S(2)}) copy-start(bf16[2,6,128,128]{2,3,1,0:T(8,128)(2,1)S(1)} %fusion.49) | copy-start | bytes 1179652
  112.5 8.4 %copy-start.13 = (bf16[1024,2,128]{2,1,0:T(2,128)(2,1)}, bf16[1024,2,128]{2,1,0:T(2,128)(2,1)S(1)}, u32[]{:S(2)}) copy-start(bf16[1024,2,128]{2,1,0:T(2,128)(2,1)S(1)} %reshape.471) | copy-start | bytes 1572868
  120.9 56.8 %copy-start.4 = (bf16[1,128,1536]{2,1,0:T(8,128)(2,1)S(1)}, bf16[1,128,1536]{2,1,0:T(8,128)(2,1)}, u32[]{:S(2)}) copy-start(bf16[1,128,1536]{2,1,0:T(8,128)(2,1)} %param.11) | copy-start | bytes 1179652
  123.7 57.2 %copy-start.7 = (bf16[2,6,128,128]{2,3,1,0:T(8,128)(2,1)}, bf16[2,6,128,128]{2,3,1,0:T(8,128)(2,1)S(1)}, u32[]{:S(2)}) copy-start(bf16[2,6,128,128]{2,3,1,0:T(8,128)(2,1)S(1)} %get-tuple-element.60) | copy-start | bytes 1179652
  180.9 12.8 %copy-start.8 = (bf16[1,128,1536]{2,1,0:T(8,128)(2,1)S(1)}, bf16[1,128,1536]{2,1,0:T(8,128)(2,1)}, u32[]{:S(2)}) copy-start(bf16[1,128,1536]{2,1,0:T(8,128)(2,1)} %param.21) | copy-start | bytes 1179652
  180.9 11.5 %copy-start.36 = (f32[128]{0:T(128)}, f32[128]{0:T(128)S(1)}, u32[]{:S(2)}) copy-start(f32[128]{0:T(128)S(1)} %add_rsqrt_fusion) | copy-start | bytes 1540
  181.1 11.3 %collective-permute-start = (bf16[128,1536]{1,0:T(8,128)(2,1)S(1)}, bf16[128,1536]{1,0:T(8,128)(2,1)S(1)}, u32[]{:S(2)}, u32[]{:S(2)}) collective-permute-start(bf16[128,1536]{1,0:T(8,128)(2,1)S(1)} %multiply_convert_fusion.4), channel_id=1, source_target_pairs={{0,1},{1,0},{2,3},{3,2},{4,5},{5,4},{6,7},{7,6},{8,9},{9,8},{10,11... | collective-permute-start | bytes 1179656 | tf_op jit(solution)/shard_map/ppermute | solution.py:66
  193.4 153.0 %all-gather.18.cloned.1.call-start = ((), (), s32[]{:S(2)}) async-start(), calls=%async_computation.16 | async-start | bytes 7077888 | tf_op jit(solution)/shard_map/all_gather | solution.py:71
  193.7 10.5 %collective-permute-start.3 = (bf16[128,1536]{1,0:T(8,128)(2,1)S(1)}, bf16[128,1536]{1,0:T(8,128)(2,1)S(1)}, u32[]{:S(2)}, u32[]{:S(2)}) collective-permute-start(bf16[128,1536]{1,0:T(8,128)(2,1)S(1)} %bitcast.262), channel_id=1, source_target_pairs={{0,1},{1,0},{2,3},{3,2},{4,5},{5,4},{6,7},{7,6},{8,9},{9,8},{10,11... | collective-permute-start | bytes 1179656 | tf_op jit(solution)/shard_map/ppermute | solution.py:66
  224.6 100.2 %all-to-all-start = ((bf16[4,2,384,560]{2,3,1,0:T(8,128)(2,1)}), bf16[4,2,384,560]{2,3,1,0:T(8,128)(2,1)}, u32[]{:S(2)}, u32[]{:S(2)}) async-start(bf16[4,2,384,560]{2,3,1,0:T(8,128)(2,1)} %pad_maximum_fusion), calls=%async_computation | async-start | bytes 6881280 | tf_op jit(solution)/shard_map/all_to_all | solution.py:132
  229.3 201.5 %reduce-scatter.6.cloned.1.call-start = ((), (), s32[]{:S(2)}) async-start(), calls=%async_computation.17 | async-start | bytes 7077888 | tf_op jit(solution)/shard_map/reduce_scatter | solution.py:75
  230.6 115.8 %copy-start.30 = (bf16[280,1536]{1,0:T(8,128)(2,1)}, bf16[280,1536]{1,0:T(8,128)(2,1)S(1)}, u32[]{:S(2)}) copy-start(bf16[280,1536]{1,0:T(8,128)(2,1)S(1)} %constant_dynamic-slice_fusion.10) | copy-start | bytes 2580484
  230.6 115.8 %collective-permute-start.1 = (bf16[280,1536]{1,0:T(8,128)(2,1)S(1)}, bf16[280,1536]{1,0:T(8,128)(2,1)}, u32[]{:S(2)}, u32[]{:S(2)}) collective-permute-start(bf16[280,1536]{1,0:T(8,128)(2,1)S(1)} %constant_dynamic-slice_fusion.10), channel_id=1, source_target_pairs={{2,0},{3,1},{0,2},{1,3},{6,4},{7,5},{4,6},{5,7},{10,8},{11,9},{8,1... | collective-permute-start | bytes 2580488 | tf_op jit(solution)/shard_map/ppermute | solution.py:139
  331.4 9.2 %copy-start.5 = (bf16[2,1024,1536]{2,1,0:T(8,128)(2,1)S(1)}, bf16[2,1024,1536]{2,1,0:T(8,128)(2,1)}, u32[]{:S(2)}) copy-start(bf16[2,1024,1536]{2,1,0:T(8,128)(2,1)} %all-gather.16.cloned.1.call-done) | copy-start | bytes 18874372
  331.4 9.2 %copy-start.15 = (bf16[70,8,4,384]{3,1,2,0:T(8,128)(2,1)S(1)}, bf16[70,8,4,384]{3,1,2,0:T(8,128)(2,1)}, u32[]{:S(2)}) copy-start(bf16[70,8,4,384]{3,1,2,0:T(8,128)(2,1)} %copy.204) | copy-start | bytes 5160964
  346.4 10.8 %copy-start.16 = (bf16[70,8,4,384]{3,1,2,0:T(8,128)(2,1)S(1)}, bf16[70,8,4,384]{3,1,2,0:T(8,128)(2,1)}, u32[]{:S(2)}) copy-start(bf16[70,8,4,384]{3,1,2,0:T(8,128)(2,1)} %copy.204) | copy-start | bytes 5160964
  369.4 250.4 %all-gather.20.cloned.1.call-start = ((), (), s32[]{:S(2)}) async-start(), calls=%async_computation.19 | async-start | bytes 3538944 | tf_op jit(solution)/shard_map/all_gather | solution.py:253
  370.2 290.5 %all-gather.22.cloned.1.call-start = ((), (), s32[]{:S(2)}) async-start(), calls=%async_computation.20 | async-start | bytes 3538944 | tf_op jit(solution)/shard_map/all_gather | solution.py:253
  370.9 298.6 %reduce-scatter.8.cloned.1.call-start = ((), (), s32[]{:S(2)}) async-start(), calls=%async_computation.18 | async-start | bytes 1179648 | tf_op jit(solution)/shard_map/reduce_scatter | solution.py:240
  431.8 10.8 %collective-permute-start.4 = (bf16[128,1536]{1,0:T(8,128)(2,1)S(1)}, bf16[128,1536]{1,0:T(8,128)(2,1)S(1)}, u32[]{:S(2)}, u32[]{:S(2)}) collective-permute-start(bf16[128,1536]{1,0:T(8,128)(2,1)S(1)} %slice_bitcast_fusion), channel_id=1, source_target_pairs={{0,1},{1,0},{2,3},{3,2},{4,5},{5,4},{6,7},{7,6},{8,9},{9,8},{10,11... | collective-permute-start | bytes 1179656 | tf_op jit(solution)/shard_map/ppermute | solution.py:66
  433.4 9.2 %copy-start.10 = (bf16[2,128,1536]{2,1,0:T(8,128)(2,1)S(1)}, bf16[2,128,1536]{2,1,0:T(8,128)(2,1)}, u32[]{:S(2)}) copy-start(bf16[2,128,1536]{2,1,0:T(8,128)(2,1)} %reduce-scatter.6.cloned.1.call-done) | copy-start | bytes 2359300
  433.4 9.2 %copy-start.37 = (f32[128]{0:T(128)S(1)}, f32[128]{0:T(128)}, u32[]{:S(2)}) copy-start(f32[128]{0:T(128)} %copy-done.36) | copy-start | bytes 1540
  471.3 122.2 %all-to-all-start.5 = ((bf16[4,2,384,560]{2,3,1,0:T(8,128)(2,1)}), bf16[4,2,384,560]{2,3,1,0:T(8,128)(2,1)}, u32[]{:S(2)}, u32[]{:S(2)}) async-start(bf16[4,2,384,560]{2,3,1,0:T(8,128)(2,1)} %copy.169), calls=%async_computation.8 | async-start | bytes 6881280 | tf_op jit(solution)/shard_map/all_to_all | solution.py:200
  476.2 211.4 %reduce-scatter.4.cloned.1.call-start = ((), (), s32[]{:S(2)}) async-start(), calls=%async_computation.15 | async-start | bytes 7077888 | tf_op jit(solution)/shard_map/reduce_scatter | solution.py:75
  493.3 95.9 %collective-permute-start.5 = (bf16[280,1536]{1,0:T(8,128)(2,1)S(1)}, bf16[280,1536]{1,0:T(8,128)(2,1)S(1)}, u32[]{:S(2)}, u32[]{:S(2)}) collective-permute-start(bf16[280,1536]{1,0:T(8,128)(2,1)S(1)} %slice.196), channel_id=1, source_target_pairs={{0,2},{1,3},{2,0},{3,1},{4,6},{5,7},{6,4},{7,5},{8,10},{9,11},{10,... | collective-permute-start | bytes 2580488 | tf_op jit(solution)/shard_map/ppermute | solution.py:220
  593.5 21.9 %all-to-all-start.7 = ((bf16[8,280,192]{2,1,0:T(8,128)(2,1)}), bf16[8,280,192]{2,1,0:T(8,128)(2,1)S(1)}, u32[]{:S(2)}, u32[]{:S(2)}) async-start(bf16[8,280,192]{2,1,0:T(8,128)(2,1)} %bitcast.245), calls=%async_computation.10 | async-start | bytes 2293760 | tf_op jit(solution)/shard_map/all_to_all | solution.py:221
  615.5 26.9 %all-to-all-start.6 = ((bf16[8,1,384,280]{2,3,1,0:T(8,128)(2,1)}), bf16[8,1,384,280]{2,3,1,0:T(8,128)(2,1)}, u32[]{:S(2)}, u32[]{:S(2)}) async-start(bf16[8,1,384,280]{2,3,1,0:T(8,128)(2,1)} %bitcast.249), calls=%async_computation.9 | async-start | bytes 3440640 | tf_op jit(solution)/shard_map/all_to_all | solution.py:212
  629.0 21.8 %copy-start.12 = (bf16[1024,2,128,1]{0,2,3,1:T(8,128)(2,1)S(1)}, bf16[1024,2,128,1]{0,2,3,1:T(8,128)(2,1)}, u32[]{:S(2)}) copy-start(bf16[1024,2,128,1]{0,2,3,1:T(8,128)(2,1)} %copy-done.11) | copy-start | bytes 1572868
  646.7 12.4 %all-to-all-start.3 = ((bf16[8,128,192]{1,2,0:T(8,128)(2,1)}), bf16[8,128,192]{1,2,0:T(8,128)(2,1)}, u32[]{:S(2)}, u32[]{:S(2)}) async-start(bf16[8,128,192]{1,2,0:T(8,128)(2,1)} %bitcast.68), calls=%async_computation.6 | async-start | bytes 786432 | tf_op jit(solution)/shard_map/all_to_all | solution.py:255
  660.6 10.8 %copy-start.33 = (f32[128,128]{1,0:T(8,128)S(1)}, f32[128,128]{1,0:T(8,128)}, u32[]{:S(2)}) copy-start(f32[128,128]{1,0:T(8,128)} %copy-done.32) | copy-start | bytes 196612
  664.6 8.5 %copy-start.18 = (bf16[128,1536]{0,1:T(8,128)(2,1)S(1)}, bf16[128,1536]{0,1:T(8,128)(2,1)}, u32[]{:S(2)}) copy-start(bf16[128,1536]{0,1:T(8,128)(2,1)} %fusion.35) | copy-start | bytes 1179652
  664.6 19.6 %all-to-all-start.4 = ((bf16[4,384,192]{1,2,0:T(8,128)(2,1)}), bf16[4,384,192]{1,2,0:T(8,128)(2,1)S(1)}, u32[]{:S(2)}, u32[]{:S(2)}) async-start(bf16[4,384,192]{1,2,0:T(8,128)(2,1)} %fusion.76), calls=%async_computation.7 | async-start | bytes 1179648 | tf_op jit(solution)/shard_map/all_to_all | solution.py:259
  684.1 13.1 %all-to-all-start.1 = ((bf16[8,128,256]{2,1,0:T(8,128)(2,1)}), bf16[8,128,256]{2,1,0:T(8,128)(2,1)S(1)}, u32[]{:S(2)}, u32[]{:S(2)}) async-start(bf16[8,128,256]{2,1,0:T(8,128)(2,1)} %bitcast.60), calls=%async_computation.4 | async-start | bytes 1048576 | tf_op jit(solution)/shard_map/all_to_all | solution.py:255
  689.4 63.2 %collective-permute-start.2 = (bf16[128,1536]{1,0:T(8,128)(2,1)}, bf16[128,1536]{1,0:T(8,128)(2,1)}, u32[]{:S(2)}, u32[]{:S(2)}) collective-permute-start(bf16[128,1536]{1,0:T(8,128)(2,1)} %slice_bitcast_fusion.2), channel_id=1, source_target_pairs={{0,1},{1,0},{2,3},{3,2},{4,5},{5,4},{6,7},{7,6},{8,9},{9,8},{10,11... | collective-permute-start | bytes 1179656 | tf_op jit(solution)/shard_map/ppermute | solution.py:66
  701.0 54.7 %all-to-all-start.2 = ((bf16[4,384,256]{2,1,0:T(8,128)(2,1)}), bf16[4,384,256]{2,1,0:T(8,128)(2,1)}, u32[]{:S(2)}, u32[]{:S(2)}) async-start(bf16[4,384,256]{2,1,0:T(8,128)(2,1)} %fusion.75), calls=%async_computation.5 | async-start | bytes 1572864 | tf_op jit(solution)/shard_map/all_to_all | solution.py:259
  705.3 47.3 %copy-start.38 = (f32[128]{0:T(128)S(1)}, f32[128]{0:T(128)}, u32[]{:S(2)}) copy-start(f32[128]{0:T(128)} %copy-done.36) | copy-start | bytes 1540
  705.3 47.3 %copy-start.44 = (f32[128]{0:T(128)S(1)}, f32[128]{0:T(128)}, u32[]{:S(2)}) copy-start(f32[128]{0:T(128)} %copy-done.43) | copy-start | bytes 1540
  705.3 52.4 %copy-start.1 = (bf16[384,2048]{1,0:T(8,128)(2,1)S(1)}, bf16[384,2048]{1,0:T(8,128)(2,1)}, u32[]{:S(2)}) copy-start(bf16[384,2048]{1,0:T(8,128)(2,1)} %param.15) | copy-start | bytes 4718596
  (24 other events, 112.5 us)
Sparse Core Ops, SparseCore 0:
  11.4 71.8 all-gather.9
  88.6 21.8 all-gather.11
  114.0 63.6 all-gather.13
  193.5 43.6 all-gather.15
  239.0 45.3 all-gather.17
  369.5 61.2 reduce-scatter.5
  432.7 32.1 all-gather.19
  466.8 32.7 all-gather.21
  502.7 35.9 reduce-scatter.7
  541.9 63.7 reduce-scatter.3
